TPU v7x, 32 devices: a whole 2x2x4 slice. The times are simulated.
32 devices in a mesh: batch: 8 (over y, x, core), chan: 4 (over z).
Axes of the slice: x: 2, y: 2, z: 4, core: 2. Of those that a mesh axis runs over, the one named last changes fastest.
Arguments:
- images: bfloat16 [64, 14, 14, 4096], P('batch', None, None, 'chan'), may hold values from -12 to 12, as said below
- reduce_weight: bfloat16 [4096, 1024], P(None, 'chan'), may hold values from -0.09375 to 0.09375
- reduce_gain: float32 [1024], P('chan'), may hold values from 0.25 to 1.75
- reduce_bias: float32 [1024], P('chan'), may hold values from -0.5 to 0.5
- spatial_weight: bfloat16 [3, 3, 1024, 1024], P(None, None, None, 'chan'), may hold values from -0.0625 to 0.0625
- spatial_gain: float32 [1024], P('chan'), may hold values from 0.25 to 1.75
- spatial_bias: float32 [1024], P('chan'), may hold values from -0.5 to 0.5
- expand_weight: bfloat16 [1024, 4096], P(None, 'chan'), may hold values from -0.1875 to 0.1875
- expand_gain: float32 [4096], P('chan'), may hold values from 0.25 to 1.75
- expand_bias: float32 [4096], P('chan'), may hold values from -0.5 to 0.5
Outputs:
- block_out: bfloat16 [64, 14, 14, 4096], P('batch', None, None, 'chan')
Inputs may be any that keep to these rules, and one draw needn't show every extreme that they name: In the images, the per-channel mean and scale differ from one block of 8 images to the next.
All inputs are finite; a program needn't handle non-finite values.
Results may differ from a plain program's by a relative error of at most 0.0047.
Values may be sent and summed in bfloat16 or wider, within the bound.
A program may use at most 128 MiB of HBM per device.

v0:
```python
import jax
import jax.numpy as jnp
from jax import lax
from jax.sharding import PartitionSpec as P

eps = 0.001


def totals(parts):
    return lax.psum((parts[0],), "batch")


def batch_norm(values, gain, bias, count):
    (total,) = totals((jnp.sum(values, axis=0),))
    mean = total / count
    centred = values - mean
    (spread,) = totals((jnp.sum(centred * centred, axis=0),))
    var = spread / count
    return centred * (gain / jnp.sqrt(var + eps)) + bias


def body(
    images,
    reduce_weight,
    reduce_gain,
    reduce_bias,
    spatial_weight,
    spatial_gain,
    spatial_bias,
    expand_weight,
    expand_gain,
    expand_bias,
):
    imgs, side = (images.shape[0], images.shape[1])
    rows = imgs * side * side
    count = rows * lax.axis_size("batch")
    mid_local = reduce_weight.shape[1]
    out_local = expand_weight.shape[1]
    own_rows = lax.all_to_all(reduce_weight, "chan", split_axis=0, concat_axis=1, tiled=True)
    partial_first = jnp.dot(
        images.reshape(rows, out_local), own_rows, preferred_element_type=jnp.float32
    )
    first = lax.psum_scatter(partial_first, "chan", scatter_dimension=1, tiled=True)
    act_one = jnp.maximum(batch_norm(first, reduce_gain, reduce_bias, count), 0.0).astype(
        jnp.bfloat16
    )
    act_one = act_one.reshape(imgs, side, side, mid_local)
    total = jnp.zeros((rows, mid_local), jnp.float32)
    piece = lax.all_gather(act_one, "chan", axis=3, tiled=True)
    width = piece.shape[-1]
    padded = jnp.pad(piece, ((0, 0), (1, 1), (1, 1), (0, 0)))
    for row_tap in range(3):
        for col_tap in range(3):
            window = padded[:, row_tap : row_tap + side, col_tap : col_tap + side, :].reshape(
                rows, width
            )
            block = spatial_weight[row_tap, col_tap]
            total = total + jnp.dot(window, block, preferred_element_type=jnp.float32)
    act_two = jnp.maximum(batch_norm(total, spatial_gain, spatial_bias, count), 0.0).astype(
        jnp.bfloat16
    )
    block = expand_weight
    third = jnp.dot(
        lax.all_gather(act_two, "chan", axis=1, tiled=True),
        block,
        preferred_element_type=jnp.float32,
    )
    normed = batch_norm(third, expand_gain, expand_bias, count)
    summed = normed + images.reshape(rows, out_local).astype(jnp.float32)
    return jnp.maximum(summed, 0.0).astype(jnp.bfloat16).reshape(imgs, side, side, out_local)


def solution(mesh):
    in_specs = (
        P("batch", None, None, "chan"),
        P(None, "chan"),
        P("chan"),
        P("chan"),
        P(None, None, None, "chan"),
        P("chan"),
        P("chan"),
        P(None, "chan"),
        P("chan"),
        P("chan"),
    )
    out_specs = P("batch", None, None, "chan")
    return jax.shard_map(body, mesh=mesh, in_specs=in_specs, out_specs=out_specs, check_vma=False)
```

profile of v0, /device:TPU:0, one launch (start us, length us, event | category | flops | bytes accessed | tf_op | source)
XLA Modules:
  0.0 540.0 jit_solution(18199424458085482704)
XLA Ops:
  6.5 6.5 %all-to-all-start = ((bf16[4,1024,256]{2,1,0:T(8,128)(2,1)}), bf16[4,1024,256]{2,1,0:T(8,128)(2,1)}, u32[]{:S(2)}, u32[]{:S(2)}) async-start(bf16[4,1024,256]{2,1,0:T(8,128)(2,1)} %bitcast.45), calls=%async_computation | async-start | bytes 4194304 | tf_op jit(solution)/shard_map/all_to_all | solution.py:39
  13.0 5.5 %copy.15 = bf16[8,14,14,1024]{3,2,1,0:T(8,128)(2,1)} copy(bf16[8,14,14,1024]{3,0,2,1:T(8,128)(2,1)} %param.10) | data formatting | bytes 6422528 | tf_op args[0]
  18.5 5.6 %reshape.49 = bf16[1568,1024]{1,0:T(8,128)(2,1)} reshape(bf16[8,14,14,1024]{3,2,1,0:T(8,128)(2,1)} %copy.15) | data formatting | bytes 6422528 | tf_op jit(solution)/shard_map/reshape | solution.py:41
  24.1 37.2 %all-to-all-done = bf16[4,1024,256]{2,1,0:T(8,128)(2,1)} async-done(((bf16[4,1024,256]{2,1,0:T(8,128)(2,1)}), bf16[4,1024,256]{2,1,0:T(8,128)(2,1)}, u32[]{:S(2)}, u32[]{:S(2)}) %all-to-all-start) | async-done | bytes 2097184 | tf_op jit(solution)/shard_map/all_to_all | solution.py:39
  61.3 4.0 copy.16
  65.3 8.8 %fusion.21 = f32[1568,1024]{1,0:T(8,128)} fusion(bf16[1568,1024]{1,0:T(8,128)(2,1)} %reshape.49, bf16[1024,1024]{0,1:T(8,128)(2,1)} %bitcast.46), kind=kOutput, calls=%fused_computation.49 | convolution fusion | flops 3288334336 | bytes 11730944 | tf_op jit(solution)/shard_map/dot_general | solution.py:40
  74.1 0.0 reduce-scatter.2.cloned.1.call-update
  74.2 0.0 all-gather.3.cloned.1.call-start
  74.2 112.1 %reduce-scatter.2.cloned.1.call-done = f32[1568,256]{1,0:T(8,128)} async-done(((f32[1568,1024]{1,0:T(8,128)}), f32[1568,256]{1,0:T(8,128)}) %reduce-scatter.2.cloned.1.call-update) | async-done | bytes 1605648 | tf_op jit(solution)/shard_map/reduce_scatter | solution.py:43
  186.3 1.6 reduce_sum.54
  187.9 13.5 %psum.42 = f32[256]{0:T(256)S(1)} all-reduce(f32[256]{0:T(256)S(1)} %reduce_sum.54), channel_id=1, replica_groups=mesh['batch'=8,'chan'=4] {'batch'}, use_global_device_ids=true, to_apply=%region_2.0 | all-reduce | flops 256 | bytes 2048 | tf_op jit(solution)/shard_map/psum | solution.py:10
  201.5 1.7 multiply_reduce_fusion.2
  203.1 11.8 %psum.43 = f32[256]{0:T(256)S(1)} all-reduce(f32[256]{0:T(256)S(1)} %multiply_reduce_fusion.2), channel_id=1, replica_groups=mesh['batch'=8,'chan'=4] {'batch'}, use_global_device_ids=true, to_apply=%region_4.0 | all-reduce | flops 256 | bytes 2048 | tf_op jit(solution)/shard_map/psum | solution.py:10
  215.0 1.7 maximum_convert_fusion.2
  216.6 1.2 reshape.50
  217.8 0.2 all-gather.5.cloned.1.call-start
  218.0 70.6 %all-gather.3.cloned.1.call-done = bf16[8,14,14,1024]{3,2,1,0:T(8,128)(2,1)} async-done(((bf16[8,14,14,256]{3,2,1,0:T(8,128)(2,1)}), bf16[8,14,14,1024]{3,2,1,0:T(8,128)(2,1)}) %all-gather.3.cloned.1.call-update) | async-done | bytes 3211280 | tf_op jit(solution)/shard_map/all_gather | solution.py:49
  288.6 23.7 %pad_slice_fusion = (bf16[8,14,14,1024]{3,2,1,0:T(8,128)(2,1)}, bf16[8,14,14,1024]{3,2,1,0:T(8,128)(2,1)}, bf16[8,14,14,1024]{3,2,1,0:T(8,128)(2,1)}, bf16[8,14,...) fusion(bf16[8,14,14,1024]{3,2,1,0:T(8,128)(2,1)} %all-gather.3., ...), kind=kLoop, calls=%fused_computation.10 | loop fusion | bytes 28901376 | tf_op jit(solution)/shard_map/slice | solution.py:54
  312.3 5.7 %reshape.59 = bf16[1568,1024]{1,0:T(8,128)(2,1)} reshape(bf16[8,14,14,1024]{3,2,1,0:T(8,128)(2,1)} %get-tuple-element.5) | data formatting | bytes 6422528 | tf_op jit(solution)/shard_map/reshape | solution.py:54
  318.1 5.7 %reshape.52 = bf16[1568,1024]{1,0:T(8,128)(2,1)} reshape(bf16[8,14,14,1024]{3,2,1,0:T(8,128)(2,1)} %get-tuple-element.6) | data formatting | bytes 6422528 | tf_op jit(solution)/shard_map/reshape | solution.py:54
  323.7 5.6 %reshape.53 = bf16[1568,1024]{1,0:T(8,128)(2,1)} reshape(bf16[8,14,14,1024]{3,2,1,0:T(8,128)(2,1)} %get-tuple-element.7) | data formatting | bytes 6422528 | tf_op jit(solution)/shard_map/reshape | solution.py:54
  329.4 5.7 %reshape.54 = bf16[1568,1024]{1,0:T(8,128)(2,1)} reshape(bf16[8,14,14,1024]{3,2,1,0:T(8,128)(2,1)} %get-tuple-element.8) | data formatting | bytes 6422528 | tf_op jit(solution)/shard_map/reshape | solution.py:54
  335.0 5.7 %reshape.56 = bf16[1568,1024]{1,0:T(8,128)(2,1)} reshape(bf16[8,14,14,1024]{3,2,1,0:T(8,128)(2,1)} %get-tuple-element.9) | data formatting | bytes 6422528 | tf_op jit(solution)/shard_map/reshape | solution.py:54
  340.7 5.6 %reshape.57 = bf16[1568,1024]{1,0:T(8,128)(2,1)} reshape(bf16[8,14,14,1024]{3,2,1,0:T(8,128)(2,1)} %get-tuple-element.10) | data formatting | bytes 6422528 | tf_op jit(solution)/shard_map/reshape | solution.py:54
  346.3 5.6 %reshape.58 = bf16[1568,1024]{1,0:T(8,128)(2,1)} reshape(bf16[8,14,14,1024]{3,2,1,0:T(8,128)(2,1)} %get-tuple-element.11) | data formatting | bytes 6422528 | tf_op jit(solution)/shard_map/reshape | solution.py:54
  352.0 5.7 %reshape.51 = bf16[1568,1024]{1,0:T(8,128)(2,1)} reshape(bf16[8,14,14,1024]{3,2,1,0:T(8,128)(2,1)} %get-tuple-element.12) | data formatting | bytes 6422528 | tf_op jit(solution)/shard_map/reshape | solution.py:54
  357.6 3.2 fusion.8
  360.8 2.2 convolution_add_fusion.7
  363.0 2.2 convolution_add_fusion.6
  365.3 3.3 convolution_add_fusion.5
  368.5 5.6 %reshape.55 = bf16[1568,1024]{1,0:T(8,128)(2,1)} reshape(bf16[8,14,14,1024]{3,2,1,0:T(8,128)(2,1)} %all-gather.3.cloned.1.call-done) | data formatting | bytes 6422528 | tf_op jit(solution)/shard_map/reshape | solution.py:54
  374.2 3.7 convolution_add_fusion.4
  377.9 2.2 convolution_add_fusion.3
  380.1 2.2 convolution_add_fusion.2
  382.3 2.2 convolution_add_fusion.1
  384.6 3.3 fusion.19
  387.8 13.6 %psum.44 = f32[256]{0:T(256)S(1)} all-reduce(f32[256]{0:T(256)S(1)} %get-tuple-element.13), channel_id=1, replica_groups=mesh['batch'=8,'chan'=4] {'batch'}, use_global_device_ids=true, to_apply=%region_6.7 | all-reduce | flops 256 | bytes 2048 | tf_op jit(solution)/shard_map/psum | solution.py:10
  401.5 1.7 multiply_reduce_fusion.1
  403.1 11.8 %psum.45 = f32[256]{0:T(256)S(1)} all-reduce(f32[256]{0:T(256)S(1)} %multiply_reduce_fusion.1), channel_id=1, replica_groups=mesh['batch'=8,'chan'=4] {'batch'}, use_global_device_ids=true, to_apply=%region_8.9 | all-reduce | flops 256 | bytes 2048 | tf_op jit(solution)/shard_map/psum | solution.py:10
  414.9 2.6 maximum_convert_fusion.1
  417.5 61.0 %all-gather.5.cloned.1.call-done = bf16[1568,1024]{1,0:T(8,128)(2,1)} async-done(((bf16[1568,256]{1,0:T(8,128)(2,1)}), bf16[1568,1024]{1,0:T(8,128)(2,1)}) %all-gather.5.cloned.1.call-update) | async-done | bytes 3211280 | tf_op jit(solution)/shard_map/all_gather | solution.py:64
  478.5 7.4 %fusion.20 = (f32[1024]{0:T(1024)S(1)}, f32[1568,1024]{1,0:T(8,128)}) fusion(bf16[1568,1024]{1,0:T(8,128)(2,1)} %all-gather.5.cloned.1.call-done, bf16[1024,1024]{1,0:T(8,128)(2,1)S(1)} %copy-done), kind=kOutput, calls=%fused_computation.48 | convolution fusion | flops 3289938944 | bytes 11735040 | tf_op jit(solution)/shard_map/dot_general | solution.py:63
  485.9 13.6 %psum.46 = f32[1024]{0:T(1024)S(1)} all-reduce(f32[1024]{0:T(1024)S(1)} %get-tuple-element.15), channel_id=1, replica_groups=mesh['batch'=8,'chan'=4] {'batch'}, use_global_device_ids=true, to_apply=%region_10.11 | all-reduce | flops 1024 | bytes 8192 | tf_op jit(solution)/shard_map/psum | solution.py:10
  499.5 3.5 multiply_reduce_fusion
  503.1 11.8 %psum.47 = f32[1024]{0:T(1024)S(1)} all-reduce(f32[1024]{0:T(1024)S(1)} %multiply_reduce_fusion), channel_id=1, replica_groups=mesh['batch'=8,'chan'=4] {'batch'}, use_global_device_ids=true, to_apply=%region_12.13 | all-reduce | flops 1024 | bytes 8192 | tf_op jit(solution)/shard_map/psum | solution.py:10
  514.9 7.0 %maximum_convert_fusion = bf16[1568,1024]{1,0:T(8,128)(2,1)} fusion(bf16[1568,1024]{1,0:T(8,128)(2,1)} %reshape.49, f32[1568,1024]{1,0:T(8,128)} %get-tuple-element.16, f32[1024]{0:T(1024)S(1)} %copy-done.8, f32[1024]{0:T(1024)S(1)} %rsqrt_multiply_fusion, f32[1024]{0:T(1024)S(1)} %broadcast_multiply_fusion), kind=kLoop, calls=%fused_computation | loop fusion | flops 11239424 | bytes 12857344 | tf_op jit(solution)/shard_map/convert_element_type | solution.py:70
  521.8 5.6 %reshape.60 = bf16[8,14,14,1024]{3,2,1,0:T(8,128)(2,1)} reshape(bf16[1568,1024]{1,0:T(8,128)(2,1)} %maximum_convert_fusion) | data formatting | bytes 6422528 | tf_op jit(solution)/shard_map/reshape | solution.py:70
  527.5 6.0 %copy.17 = bf16[8,14,14,1024]{3,0,2,1:T(8,128)(2,1)} copy(bf16[8,14,14,1024]{3,2,1,0:T(8,128)(2,1)} %reshape.60) | data formatting | bytes 6422528 | tf_op jit(solution)/shard_map/reshape | solution.py:70
  (37 shorter events, 0.1 us)
Async XLA Ops:
  6.5 471.9 %copy-start = (bf16[1024,1024]{1,0:T(8,128)(2,1)S(1)}, bf16[1024,1024]{1,0:T(8,128)(2,1)}, u32[]{:S(2)}) copy-start(bf16[1024,1024]{1,0:T(8,128)(2,1)} %param.17) | copy-start | bytes 6291460
  6.5 54.8 %all-to-all-start = ((bf16[4,1024,256]{2,1,0:T(8,128)(2,1)}), bf16[4,1024,256]{2,1,0:T(8,128)(2,1)}, u32[]{:S(2)}, u32[]{:S(2)}) async-start(bf16[4,1024,256]{2,1,0:T(8,128)(2,1)} %bitcast.45), calls=%async_computation | async-start | bytes 4194304 | tf_op jit(solution)/shard_map/all_to_all | solution.py:39
  13.0 173.3 %reduce-scatter.2.cloned.1.call-start = ((), (), s32[]{:S(2)}) async-start(), calls=%async_computation.2 | async-start | bytes 8028160 | tf_op jit(solution)/shard_map/reduce_scatter | solution.py:43
  74.1 140.8 %copy-start.12 = (f32[256]{0:T(256)S(1)}, f32[256]{0:T(256)}, u32[]{:S(2)}) copy-start(f32[256]{0:T(256)} %param.12) | copy-start | bytes 3076
  74.1 140.8 %copy-start.10 = (f32[256]{0:T(256)S(1)}, f32[256]{0:T(256)}, u32[]{:S(2)}) copy-start(f32[256]{0:T(256)} %param.13) | copy-start | bytes 3076
  74.2 214.5 %all-gather.3.cloned.1.call-start = ((), (), s32[]{:S(2)}) async-start(), calls=%async_computation.3 | async-start | bytes 4587520 | tf_op jit(solution)/shard_map/all_gather | solution.py:49
  217.8 260.7 %all-gather.5.cloned.1.call-start = ((), (), s32[]{:S(2)}) async-start(), calls=%async_computation.4 | async-start | bytes 4014080 | tf_op jit(solution)/shard_map/all_gather | solution.py:64
  357.6 3.2 copy-start.7
  360.8 2.2 copy-start.6
  363.0 2.2 copy-start.5
  374.2 3.7 copy-start.4
  377.9 2.2 copy-start.3
  380.1 2.2 copy-start.2
  382.3 2.2 copy-start.1
  384.5 30.4 %copy-start.13 = (f32[256]{0:T(256)S(1)}, f32[256]{0:T(256)}, u32[]{:S(2)}) copy-start(f32[256]{0:T(256)} %param.15) | copy-start | bytes 3076
  384.6 30.4 %copy-start.11 = (f32[256]{0:T(256)S(1)}, f32[256]{0:T(256)}, u32[]{:S(2)}) copy-start(f32[256]{0:T(256)} %param.16) | copy-start | bytes 3076
  499.5 15.4 %copy-start.9 = (f32[1024]{0:T(1024)S(1)}, f32[1024]{0:T(1024)}, u32[]{:S(2)}) copy-start(f32[1024]{0:T(1024)} %param.18) | copy-start | bytes 12292
  499.5 15.4 %copy-start.8 = (f32[1024]{0:T(1024)S(1)}, f32[1024]{0:T(1024)}, u32[]{:S(2)}) copy-start(f32[1024]{0:T(1024)} %param.19) | copy-start | bytes 12292
Sparse Core Ops, SparseCore 0:
  74.3 111.9 reduce-scatter.1
  217.9 70.6 all-gather.2
  417.6 60.7 all-gather.4
where the time goes:
time: 542 us; the launch traced here: 540 us
  waiting for transfers between devices  281 us (52%)
  local copies, waits for them, and re-layouts  103 us (19%)
  blocking collectives  76.2 us (14%)
  matrix products  40.5 us (7%)
  other arithmetic  19.7 us (4%)
  between operations  13.3 us (2%)
  starting transfers between devices  6.74 us (1%)
    reduce_scatter x1, waiting for transfers between devices, body(): lax.psum_scatter(partial_first, 'chan', scatter_dimension=1, tiled=True)  112 us
    psum x6, blocking collectives, totals(): return lax.psum((parts[0],), 'batch')  76.2 us
    all_gather x1, waiting for transfers between devices, body(): piece = lax.all_gather(act_one, 'chan', axis=3, tiled=True)  70.6 us
    all_gather x1, waiting for transfers between devices, body(): lax.all_gather(act_two, 'chan', axis=1, tiled=True)  61 us
    reshape x9, local copies, waits for them, and re-layouts, body(): padded[:, row_tap:row_tap + side, col_tap:col_tap + side, :]  50.9 us
    all_to_all x1, waiting for transfers between devices, body(): lax.all_to_all(reduce_weight, 'chan', split_axis=0, concat_axis=1, tiled=...  37.2 us
    dot_general x9, matrix products, body(): total = total + jnp.dot(window, block, preferred_element_type=jnp.float32)  24.4 us
    slice x1, local copies, waits for them, and re-layouts, body(): padded[:, row_tap:row_tap + side, col_tap:col_tap + side, :]  23.7 us
  transfers between devices with their start and end apart: 4, of which 4 were waited for; matrix products, arithmetic and copies ran while one was open for 2% of the time, Pallas kernels for 0%

commit v1 on v0

v1 whole, which is shorter than its diff:
```python
import functools

import jax
import jax.numpy as jnp
from jax import lax
from jax.experimental import pallas as pl
from jax.experimental.pallas import tpu as pltpu
from jax.sharding import PartitionSpec as P

eps = 0.001
MESH = pl.DeviceIdType.MESH
LIMIT = 63 * 1024 * 1024


def remote(src, dst, send, recv, device):
    return pltpu.make_async_remote_copy(
        src_ref=src, dst_ref=dst, send_sem=send, recv_sem=recv,
        device_id=device, device_id_type=MESH,
    )


def greet(n, nb, z, b):
    barrier = pltpu.get_barrier_semaphore()
    for off in range(1, n):
        pl.semaphore_signal(
            barrier, inc=1, device_id={"chan": lax.rem(z + off, n)}, device_id_type=MESH
        )
    for off in range(1, nb):
        pl.semaphore_signal(
            barrier, inc=1, device_id={"batch": lax.rem(b + off, nb)}, device_id_type=MESH
        )
    pl.semaphore_wait(barrier, n + nb - 2)


def share_stats(nb, b, stat_in, send, recv):
    for off in range(1, nb):
        peer = lax.rem(b + off, nb)
        remote(
            stat_in.at[b], stat_in.at[b], send.at[off], recv.at[b], {"batch": peer}
        ).start()
    for off in range(1, nb):
        peer = lax.rem(b + off, nb)
        remote(
            stat_in.at[b], stat_in.at[peer], send.at[off], recv.at[peer], {"batch": peer}
        ).wait()


def combine(stats, local):
    nb = stats.shape[0]
    means = stats[..., 0:1, :]
    mean = jnp.sum(means, axis=0) / nb
    away = means - mean[None]
    spread = jnp.sum(stats[..., 1:2, :], axis=0) + local * jnp.sum(away * away, axis=0)
    return mean, spread / (local * nb)


def first_kernel(
    n, nb, parts, img_ref, w_ref, gb_ref, out_ref,
    wown, part, pre_in, suf_in, pre_out, suf_out, gb_in, shift, acc1, acc2, stat_in,
    w1_send, w1_recv, w2_send, w2_recv, w3_send, w3_recv, gb_send, gb_recv,
    pre_send, pre_recv, suf_send, suf_recv, st_send, st_recv,
):
    z, b = lax.axis_index("chan"), lax.axis_index("batch")
    depth = img_ref.shape[2]
    height = img_ref.shape[1]
    strip = depth // nb
    half = nb // 2
    chunks = n * parts
    partner = b + 1 - 2 * lax.rem(b, 2)
    parity = lax.rem(b, 2)
    greet(n, nb, z, b)

    def rows_of(who):
        return pl.ds(pl.multiple_of(who * strip, 16), strip)

    for off in range(1, n):
        to = lax.rem(z + off, n)
        src = w_ref.at[pl.ds(pl.multiple_of(to * depth + b * strip, 16), strip), :]
        remote(
            src, wown.at[z, rows_of(b), :], w1_send.at[off], w1_recv.at[z], {"chan": to}
        ).start()
    gb_in[z] = gb_ref[...]
    for off in range(1, n):
        to = lax.rem(z + off, n)
        remote(gb_ref, gb_in.at[z], gb_send.at[off], gb_recv.at[z], {"chan": to}).start()

    wown[z] = w_ref[pl.ds(pl.multiple_of(z * depth, 16), depth), :]

    @pl.when(z == 0)
    def _():
        pre_in[...] = jnp.zeros_like(pre_in)

    @pl.when(z == n - 1)
    def _():
        suf_in[...] = jnp.zeros_like(suf_in)

    def strip_copy(g, who, send, recv, device):
        ref = wown.at[g, rows_of(who), :]
        return remote(ref, ref, send, recv, device)

    for off in range(1, n):
        g = lax.rem(z + off, n)
        strip_copy(g, b, w1_send.at[0], w1_recv.at[g], {"chan": g}).wait_recv()
        for hop in range(1, half):
            peer = lax.rem(b + 2 * hop, nb)
            strip_copy(g, b, w2_send.at[off, hop], w2_recv.at[g, b], {"batch": peer}).start()
        strip_copy(g, b, w3_send.at[off, 0], w3_recv.at[g, b], {"batch": partner}).start()
    for off in range(1, n):
        g = lax.rem(z + off, n)
        for hop in range(1, half):
            peer = lax.rem(b + 2 * hop, nb)
            strip_copy(g, peer, w2_send.at[0, 0], w2_recv.at[g, peer], {"batch": peer}).wait_recv()
            strip_copy(
                g, peer, w3_send.at[off, hop], w3_recv.at[g, peer], {"batch": partner}
            ).start()
    for off in range(1, n):
        g = lax.rem(z + off, n)
        for hop in range(half):
            who = 2 * hop + 1 - parity
            strip_copy(g, who, w3_send.at[0, 0], w3_recv.at[g, who], {"batch": partner}).wait_recv()

    def right_copy(k):
        return remote(
            pre_out.at[k], pre_in.at[k], pre_send.at[k], pre_recv.at[k],
            {"chan": lax.rem(z + 1, n)},
        )

    def left_copy(k):
        return remote(
            suf_out.at[k], suf_in.at[k], suf_send.at[k], suf_recv.at[k],
            {"chan": lax.rem(z + n - 1, n)},
        )

    def step(s, carry):
        @pl.when(s < chunks)
        def _():
            g, r = lax.div(s, parts), lax.rem(s, parts)
            part[s] = jnp.dot(img_ref[r], wown[g], preferred_element_type=jnp.float32)

        kp = s - z

        @pl.when(jnp.logical_and(kp >= 0, kp < chunks))
        def _():
            @pl.when(z > 0)
            def _():
                right_copy(kp).wait_recv()

            @pl.when(z < n - 1)
            def _():
                pre_out[kp] = (part[kp] + pre_in[kp].astype(jnp.float32)).astype(jnp.bfloat16)
                right_copy(kp).start()

        ks = s - (n - 1 - z)

        @pl.when(jnp.logical_and(ks >= 0, ks < chunks))
        def _():
            @pl.when(z < n - 1)
            def _():
                left_copy(ks).wait_recv()

            @pl.when(z > 0)
            def _():
                suf_out[ks] = (part[ks] + suf_in[ks].astype(jnp.float32)).astype(jnp.bfloat16)
                left_copy(ks).start()

        kf = s - jnp.maximum(z, n - 1 - z)

        @pl.when(jnp.logical_and(kf >= 0, kf < chunks))
        def _():
            g, r = lax.div(kf, parts), lax.rem(kf, parts)
            value = (
                part[kf] + pre_in[kf].astype(jnp.float32) + suf_in[kf].astype(jnp.float32)
            )
            part[kf] = value

            @pl.when(r == 0)
            def _():
                shift[g] = jnp.sum(value, axis=0, keepdims=True) / height
                acc1[g] = jnp.zeros_like(acc1[g])
                acc2[g] = jnp.zeros_like(acc2[g])

            moved = value - shift[g]
            acc1[g] += jnp.sum(moved, axis=0, keepdims=True)
            acc2[g] += jnp.sum(moved * moved, axis=0, keepdims=True)

        return carry

    lax.fori_loop(0, chunks + n - 1, step, 0)

    local = height * parts
    extra = acc1[...] / local
    stat_in[b, :, 0:1, :] = shift[...] + extra
    stat_in[b, :, 1:2, :] = acc2[...] - acc1[...] * extra
    share_stats(nb, b, stat_in, st_send, st_recv)
    for off in range(1, n):
        g = lax.rem(z + off, n)
        remote(gb_ref, gb_in.at[g], gb_send.at[off], gb_recv.at[g], {"chan": g}).wait()
    mean, var = combine(stat_in[...], local)
    scale = gb_in[:, 0:1, :] / jnp.sqrt(var + eps)
    bias = gb_in[:, 1:2, :]
    width = part.shape[2]

    def finish(r, carry):
        for g in range(n):
            value = (part[g * parts + r] - mean[g]) * scale[g] + bias[g]
            out_ref[r, :, g * width : (g + 1) * width] = jnp.maximum(value, 0.0).astype(
                jnp.bfloat16
            )
        return carry

    lax.fori_loop(0, parts, finish, 0)

    for off in range(1, n):
        to = lax.rem(z + off, n)
        src = w_ref.at[pl.ds(pl.multiple_of(to * depth + b * strip, 16), strip), :]
        remote(
            src, wown.at[z, rows_of(b), :], w1_send.at[off], w1_recv.at[z], {"chan": to}
        ).wait_send()
        g = to
        for hop in range(1, half):
            peer = lax.rem(b + 2 * hop, nb)
            strip_copy(g, b, w2_send.at[off, hop], w2_recv.at[g, b], {"batch": peer}).wait_send()
        for hop in range(half):
            peer = lax.rem(b + 2 * hop, nb)
            strip_copy(
                g, peer, w3_send.at[off, hop], w3_recv.at[g, peer], {"batch": partner}
            ).wait_send()

    def drain(k, carry):
        @pl.when(z < n - 1)
        def _():
            right_copy(k).wait_send()

        @pl.when(z > 0)
        def _():
            left_copy(k).wait_send()

        return carry

    lax.fori_loop(0, chunks, drain, 0)


def third_kernel(
    n, nb, sec_ref, gb_ref, w_ref, gain_ref, out_ref, norm_ref,
    act, stat2, stat3,
    right_send, left_send, recv, s2_send, s2_recv, s3_send, s3_recv,
):
    z, b = lax.axis_index("chan"), lax.axis_index("batch")
    parts, height, width = sec_ref.shape
    local = parts * height
    greet(n, nb, z, b)
    values = sec_ref[...]
    own = jnp.sum(jnp.sum(values, axis=0), axis=0, keepdims=True) / local
    away = values - own[None]
    stat2[b, 0:1, :] = own
    stat2[b, 1:2, :] = jnp.sum(jnp.sum(away * away, axis=0), axis=0, keepdims=True)
    share_stats(nb, b, stat2, s2_send, s2_recv)
    mean, var = combine(stat2[...], local)
    scale = gb_ref[0:1, :] / jnp.sqrt(var + eps)
    bias = gb_ref[1:2, :]

    def right_copy(g, r):
        ref = act.at[g, r]
        return remote(
            ref, ref, right_send.at[g, r], recv.at[g, r], {"chan": lax.rem(z + 1, n)}
        )

    def left_copy(g, r):
        ref = act.at[g, r]
        return remote(
            ref, ref, left_send.at[g, r], recv.at[g, r], {"chan": lax.rem(z + n - 1, n)}
        )

    def rows_of(g):
        return pl.ds(pl.multiple_of(g * width, 128), width)

    def begin(r, carry):
        value = (sec_ref[r] - mean) * scale + bias
        act[z, r] = jnp.maximum(value, 0.0).astype(jnp.bfloat16)

        @pl.when(z < n - 1)
        def _():
            right_copy(z, r).start()

        @pl.when(z > 0)
        def _():
            left_copy(z, r).start()

        out_ref[r] = jnp.dot(act[z, r], w_ref[rows_of(z), :], preferred_element_type=jnp.float32)
        return carry

    lax.fori_loop(0, parts, begin, 0)

    def relay(s, carry):
        d, r = lax.div(s, parts) + 1, lax.rem(s, parts)
        g = z - d

        @pl.when(g >= 0)
        def _():
            right_copy(g, r).wait_recv()

            @pl.when(z < n - 1)
            def _():
                right_copy(g, r).start()

            out_ref[r] += jnp.dot(
                act[g, r], w_ref[rows_of(g), :], preferred_element_type=jnp.float32
            )

        h = z + d

        @pl.when(h < n)
        def _():
            left_copy(h, r).wait_recv()

            @pl.when(z > 0)
            def _():
                left_copy(h, r).start()

            out_ref[r] += jnp.dot(
                act[h, r], w_ref[rows_of(h), :], preferred_element_type=jnp.float32
            )

        return carry

    lax.fori_loop(0, parts * (n - 1), relay, 0)

    def add(r, carry):
        return carry + jnp.sum(out_ref[r], axis=0, keepdims=True)

    zero = jnp.zeros((1, out_ref.shape[2]), jnp.float32)
    own3 = lax.fori_loop(0, parts, add, zero) / local

    def add_square(r, carry):
        away = out_ref[r] - own3
        return carry + jnp.sum(away * away, axis=0, keepdims=True)

    stat3[b, 0:1, :] = own3
    stat3[b, 1:2, :] = lax.fori_loop(0, parts, add_square, zero)
    share_stats(nb, b, stat3, s3_send, s3_recv)
    mean3, var3 = combine(stat3[...], local)
    norm_ref[0:1, :] = mean3
    norm_ref[1:2, :] = gain_ref[...] / jnp.sqrt(var3 + eps)

    def drain(s, carry):
        g, r = lax.div(s, parts), lax.rem(s, parts)

        @pl.when(jnp.logical_and(z < n - 1, g <= z))
        def _():
            right_copy(g, r).wait_send()

        @pl.when(jnp.logical_and(z > 0, g >= z))
        def _():
            left_copy(g, r).wait_send()

        return carry

    lax.fori_loop(0, n * parts, drain, 0)


def parts_of(rows):
    for parts in (7, 4, 2):
        if rows % (parts * 16) == 0:
            return parts
    return 1


def body(
    images,
    reduce_weight,
    reduce_gain,
    reduce_bias,
    spatial_weight,
    spatial_gain,
    spatial_bias,
    expand_weight,
    expand_gain,
    expand_bias,
):
    imgs, side = (images.shape[0], images.shape[1])
    rows = imgs * side * side
    n, nb = lax.axis_size("chan"), lax.axis_size("batch")
    mid_local = reduce_weight.shape[1]
    mid = mid_local * n
    depth = images.shape[3]
    out_local = expand_weight.shape[1]
    parts = parts_of(rows)
    height = rows // parts
    chunks = n * parts
    dma, f32, bf16 = pltpu.SemaphoreType.DMA, jnp.float32, jnp.bfloat16
    vmem = pl.BlockSpec(memory_space=pltpu.VMEM)
    flat = images.reshape(parts, height, depth)
    act_one = pl.pallas_call(
        functools.partial(first_kernel, n, nb, parts),
        out_shape=jax.ShapeDtypeStruct((parts, height, mid), bf16),
        in_specs=[vmem] * 3,
        out_specs=vmem,
        scratch_shapes=[
            pltpu.VMEM((n, depth, mid_local), bf16),
            pltpu.VMEM((chunks, height, mid_local), f32),
        ]
        + [pltpu.VMEM((chunks, height, mid_local), bf16)] * 4
        + [pltpu.VMEM((n, 2, mid_local), f32)]
        + [pltpu.VMEM((n, 1, mid_local), f32)] * 3
        + [pltpu.VMEM((nb, n, 2, mid_local), f32)]
        + [dma((n,)), dma((n,)), dma((n, nb // 2)), dma((n, nb)), dma((n, nb // 2)), dma((n, nb))]
        + [dma((n,)), dma((n,))]
        + [dma((chunks,))] * 4
        + [dma((nb,)), dma((nb,))],
        compiler_params=pltpu.CompilerParams(
            collective_id=0, has_side_effects=True, vmem_limit_bytes=LIMIT
        ),
        name="first",
    )(flat, reduce_weight, jnp.stack([reduce_gain, reduce_bias]))
    second = lax.conv_general_dilated(
        act_one.reshape(imgs, side, side, mid),
        spatial_weight,
        (1, 1),
        ((1, 1), (1, 1)),
        dimension_numbers=("NHWC", "HWIO", "NHWC"),
        preferred_element_type=f32,
    )
    third, norm = pl.pallas_call(
        functools.partial(third_kernel, n, nb),
        out_shape=(
            jax.ShapeDtypeStruct((parts, height, out_local), f32),
            jax.ShapeDtypeStruct((2, out_local), f32),
        ),
        in_specs=[vmem] * 4,
        out_specs=(vmem, vmem),
        scratch_shapes=[
            pltpu.VMEM((n, parts, height, mid_local), bf16),
            pltpu.VMEM((nb, 2, mid_local), f32),
            pltpu.VMEM((nb, 2, out_local), f32),
        ]
        + [dma((n, parts))] * 3
        + [dma((nb,))] * 4,
        compiler_params=pltpu.CompilerParams(
            collective_id=1, has_side_effects=True, vmem_limit_bytes=LIMIT
        ),
        name="third",
    )(
        second.reshape(parts, height, mid_local),
        jnp.stack([spatial_gain, spatial_bias]),
        expand_weight,
        expand_gain[None, :],
    )
    normed = (third.reshape(rows, out_local) - norm[0]) * norm[1] + expand_bias
    summed = normed + images.reshape(rows, out_local).astype(f32)
    return jnp.maximum(summed, 0.0).astype(bf16).reshape(imgs, side, side, out_local)


def solution(mesh):
    in_specs = (
        P("batch", None, None, "chan"),
        P(None, "chan"),
        P("chan"),
        P("chan"),
        P(None, None, None, "chan"),
        P("chan"),
        P("chan"),
        P(None, "chan"),
        P("chan"),
        P("chan"),
    )
    out_specs = P("batch", None, None, "chan")
    return jax.shard_map(body, mesh=mesh, in_specs=in_specs, out_specs=out_specs, check_vma=False)
```

time: 542 us -> 269 us (0.50)
  waiting for transfers between devices: 281 us -> 0 us
  Pallas kernels: 0 us -> 217 us
  blocking collectives: 76.2 us -> 0 us
  local copies, waits for them, and re-layouts: 103 us -> 27.1 us
  matrix products: 40.5 us -> 11 us
  between operations: 13.3 us -> 0.06 us
  starting transfers between devices: 6.74 us -> 0 us
  other arithmetic: 19.7 us -> 13.2 us
    pallas_call x0 -> x2, Pallas kernels: none -> 217 us  [the longest x1 148 us: body(): pl.pallas_call(functools.partial(first_kernel, n, nb, parts), out_shape=j...]
    all_gather x2 -> x0, waiting for transfers between devices: 132 us -> none  [the longest x1 70.6 us: body(): piece = lax.all_gather(act_one, 'chan', axis=3, tiled=True)]
    reduce_scatter x1 -> x0, waiting for transfers between devices: 112 us -> none  [body(): lax.psum_scatter(partial_first, 'chan', scatter_dimension=1, tiled=True)]
    psum x6 -> x0, blocking collectives: 76.2 us -> none  [totals(): return lax.psum((parts[0],), 'batch')]
    reshape x13 -> x4, local copies, waits for them, and re-layouts: 69.3 us -> 20.3 us  [the longest x1 7.71 us: body(): normed = (third.reshape(rows, out_local) - norm[0]) * norm[1] + expand_bias]
    dot_general x11 -> x0, matrix products: 40.5 us -> none  [the longest x9 24.4 us: body(): total = total + jnp.dot(window, block, preferred_element_type=jnp.float32)]
    all_to_all x1 -> x0, waiting for transfers between devices: 37.2 us -> none  [body(): lax.all_to_all(reduce_weight, 'chan', split_axis=0, concat_axis=1, tiled=...]
    slice x1, local copies, waits for them, and re-layouts: 23.7 us -> 0.78 us  [body(): normed = (third.reshape(rows, out_local) - norm[0]) * norm[1] + expand_bias]
  transfers between devices with their start and end apart: 4 -> 0, of which waited for: 4 -> 0; matrix products, arithmetic and copies ran while one was open for 2% -> 0% of each run, Pallas kernels for 0% -> 0%
where the time goes in v1:
time: 269 us; the launch traced here: 268 us
  Pallas kernels  217 us (81%)
  local copies, waits for them, and re-layouts  27.1 us (10%)
  other arithmetic  13.2 us (5%)
  matrix products  11 us (4%)
    pallas_call x1, Pallas kernels, body(): pl.pallas_call(functools.partial(first_kernel, n, nb, parts), out_shape=j...  148 us
    pallas_call x1, Pallas kernels, body(): pl.pallas_call(functools.partial(third_kernel, n, nb), out_shape=(jax.Sha...  69.4 us
    conv_general_dilated x1, matrix products, body(): lax.conv_general_dilated(act_one.reshape(imgs, side, side, mid), spatial_...  11 us
    convert_element_type x1, other arithmetic, body(): jnp.maximum(summed, 0.0).astype(bf16).reshape(imgs, side, side, out_local)  10.6 us
    reshape x1, local copies, waits for them, and re-layouts, body(): normed = (third.reshape(rows, out_local) - norm[0]) * norm[1] + expand_bias  7.71 us
    reshape x1, local copies, waits for them, and re-layouts, body(): act_one.reshape(imgs, side, side, mid)  5.66 us
    reshape x1, local copies, waits for them, and re-layouts, body(): flat = images.reshape(parts, height, depth)  5.64 us
    unnamed x5, local copies, waits for them, and re-layouts  5.49 us

profile of v1, /device:TPU:0, one launch (start us, length us, event | category | flops | bytes accessed | tf_op | source)
XLA Modules:
  0.0 268.3 jit_solution(6045572689515388028)
XLA Ops:
  0.0 1.3 pad_maximum_fusion.gb_ref
  1.3 1.3 pad_maximum_fusion.1.gb_ref
  2.6 5.5 %copy.20 = bf16[8,14,14,1024]{3,2,1,0:T(8,128)(2,1)} copy(bf16[8,14,14,1024]{3,0,2,1:T(8,128)(2,1)} %param.10) | data formatting | bytes 6422528 | tf_op args[0]
  8.1 5.6 %reshape.31.img_ref = bf16[7,224,1024]{2,1,0:T(8,128)(2,1)} reshape(bf16[8,14,14,1024]{3,2,1,0:T(8,128)(2,1)} %copy.20) | data formatting | bytes 6422528 | tf_op jit(solution)/shard_map/reshape | solution.py:392
  13.7 147.5 %first.1 = bf16[7,224,1024]{2,1,0:T(8,128)(2,1)} custom-call(bf16[7,224,1024]{2,1,0:T(8,128)(2,1)} %reshape.31.img_ref, bf16[4096,256]{1,0:T(8,128)(2,1)} %w_ref.2, f32[2,256]{1,0:T(2,128)} %pad_maximum_fusion.gb_ref), custom_call_target="tpu_custom_call" | custom-call | tf_op jit(solution)/shard_map/first/pallas_call | solution.py:393
  161.2 5.7 %reshape.32 = bf16[8,14,14,1024]{3,2,1,0:T(8,128)(2,1)} reshape(bf16[7,224,1024]{2,1,0:T(8,128)(2,1)} %first.1) | data formatting | bytes 6422528 | tf_op jit(solution)/shard_map/reshape | solution.py:416
  166.9 11.0 %fusion.5 = f32[8,14,14,256]{3,0,2,1:T(8,128)S(1)} fusion(bf16[3,3,1024,256]{3,2,1,0:T(8,128)(2,1)} %param.14, bf16[8,14,14,1024]{3,2,1,0:T(8,128)(2,1)} %reshape.32), kind=kOutput, calls=%fused_computation.6 | convolution fusion | flops 6710886400 | bytes 9535488 | tf_op jit(solution)/shard_map/conv_general_dilated | solution.py:415
  177.9 0.5 copy.22
  178.4 1.3 reshape.33.sec_ref
  179.8 69.4 %third.1 = (f32[7,224,1024]{2,1,0:T(8,128)}, f32[2,1024]{1,0:T(2,128)}) custom-call(f32[7,224,256]{2,1,0:T(8,128)} %reshape.33.sec_ref, f32[2,256]{1,0:T(2,128)} %pad_maximum_fusion.1.gb_ref, bf16[1024,1024]{1,0:T(8,128)(2,1)} %w_ref.3, f32[1,1024]{1,0:T(1,128)} %bitcast.10), custom_call_target="tpu_custom_call" | custom-call | tf_op jit(solution)/shard_map/third/pallas_call | solution.py:423
  249.2 0.8 fusion.7
  250.0 0.0 copy-start
  250.0 0.0 copy-start.1
  250.0 7.7 %reshape.34 = f32[8,14,14,1024]{3,2,1,0:T(8,128)} reshape(f32[7,224,1024]{2,1,0:T(8,128)} %get-tuple-element.7) | data formatting | bytes 12845056 | tf_op jit(solution)/shard_map/reshape | solution.py:448
  257.7 0.0 copy-done
  257.7 0.0 copy-done.1
  257.7 10.6 %fusion.4 = bf16[8,14,14,1024]{3,0,2,1:T(8,128)(2,1)} fusion(f32[8,14,14,1024]{3,2,1,0:T(8,128)} %reshape.34, bf16[8,14,14,1024]{3,0,2,1:T(8,128)(2,1)S(1)} %copy-done, f32[1024]{0:T(1024)S(1)} %copy-done.1, f32[1024]{0:T(1024)S(1)} %bitcast.9, f32[1024]{0:T(1024)S(1)} %bitcast.8), kind=kLoop, calls=%fused_computation.5 | loop fusion | flops 11239424 | bytes 12857344 | tf_op jit(solution)/shard_map/convert_element_type | solution.py:450
Async XLA Ops:
  250.0 7.7 %copy-start = (bf16[8,14,14,1024]{3,0,2,1:T(8,128)(2,1)S(1)}, bf16[8,14,14,1024]{3,0,2,1:T(8,128)(2,1)}, u32[]{:S(2)}) copy-start(bf16[8,14,14,1024]{3,0,2,1:T(8,128)(2,1)} %param.10) | copy-start | bytes 9633796
  250.0 7.7 %copy-start.1 = (f32[1024]{0:T(1024)S(1)}, f32[1024]{0:T(1024)}, u32[]{:S(2)}) copy-start(f32[1024]{0:T(1024)} %param.19) | copy-start | bytes 12292

commit v2 on v1

--- a/solution.py
+++ b/solution.py
@@ -10,6 +10,7 @@
 eps = 0.001
 MESH = pl.DeviceIdType.MESH
 LIMIT = 63 * 1024 * 1024
+SKEW = 3
 
 
 def remote(src, dst, send, recv, device):
@@ -98,26 +99,38 @@
         ref = wown.at[g, rows_of(who), :]
         return remote(ref, ref, send, recv, device)
 
-    for off in range(1, n):
-        g = lax.rem(z + off, n)
-        strip_copy(g, b, w1_send.at[0], w1_recv.at[g], {"chan": g}).wait_recv()
-        for hop in range(1, half):
-            peer = lax.rem(b + 2 * hop, nb)
-            strip_copy(g, b, w2_send.at[off, hop], w2_recv.at[g, b], {"batch": peer}).start()
-        strip_copy(g, b, w3_send.at[off, 0], w3_recv.at[g, b], {"batch": partner}).start()
-    for off in range(1, n):
-        g = lax.rem(z + off, n)
-        for hop in range(1, half):
-            peer = lax.rem(b + 2 * hop, nb)
-            strip_copy(g, peer, w2_send.at[0, 0], w2_recv.at[g, peer], {"batch": peer}).wait_recv()
-            strip_copy(
-                g, peer, w3_send.at[off, hop], w3_recv.at[g, peer], {"batch": partner}
-            ).start()
-    for off in range(1, n):
-        g = lax.rem(z + off, n)
-        for hop in range(half):
-            who = 2 * hop + 1 - parity
-            strip_copy(g, who, w3_send.at[0, 0], w3_recv.at[g, who], {"batch": partner}).wait_recv()
+    for g in range(n):
+
+        @pl.when(z != g)
+        def _():
+            strip_copy(g, b, w1_send.at[0], w1_recv.at[g], {"chan": g}).wait_recv()
+            for hop in range(1, half):
+                peer = lax.rem(b + 2 * hop, nb)
+                strip_copy(g, b, w2_send.at[g, hop], w2_recv.at[g, b], {"batch": peer}).start()
+            strip_copy(g, b, w3_send.at[g, 0], w3_recv.at[g, b], {"batch": partner}).start()
+
+    def forward(g):
+        @pl.when(z != g)
+        def _():
+            for hop in range(1, half):
+                peer = lax.rem(b + 2 * hop, nb)
+                strip_copy(
+                    g, peer, w2_send.at[g, 0], w2_recv.at[g, peer], {"batch": peer}
+                ).wait_recv()
+                strip_copy(
+                    g, peer, w3_send.at[g, hop], w3_recv.at[g, peer], {"batch": partner}
+                ).start()
+
+    def complete(g):
+        @pl.when(z != g)
+        def _():
+            for hop in range(half):
+                who = 2 * hop + 1 - parity
+                strip_copy(
+                    g, who, w3_send.at[g, 0], w3_recv.at[g, who], {"batch": partner}
+                ).wait_recv()
+
+    forward(0)
 
     def right_copy(k):
         return remote(
@@ -135,9 +148,18 @@
         @pl.when(s < chunks)
         def _():
             g, r = lax.div(s, parts), lax.rem(s, parts)
+
+            @pl.when(r == 0)
+            def _():
+                complete(g)
+
+            @pl.when(jnp.logical_and(r == parts // 2, g < n - 1))
+            def _():
+                forward(g + 1)
+
             part[s] = jnp.dot(img_ref[r], wown[g], preferred_element_type=jnp.float32)
 
-        kp = s - z
+        kp = s - SKEW * z
 
         @pl.when(jnp.logical_and(kp >= 0, kp < chunks))
         def _():
@@ -150,7 +172,7 @@
                 pre_out[kp] = (part[kp] + pre_in[kp].astype(jnp.float32)).astype(jnp.bfloat16)
                 right_copy(kp).start()
 
-        ks = s - (n - 1 - z)
+        ks = s - SKEW * (n - 1 - z)
 
         @pl.when(jnp.logical_and(ks >= 0, ks < chunks))
         def _():
@@ -163,7 +185,7 @@
                 suf_out[ks] = (part[ks] + suf_in[ks].astype(jnp.float32)).astype(jnp.bfloat16)
                 left_copy(ks).start()
 
-        kf = s - jnp.maximum(z, n - 1 - z)
+        kf = s - SKEW * jnp.maximum(z, n - 1 - z)
 
         @pl.when(jnp.logical_and(kf >= 0, kf < chunks))
         def _():
@@ -185,7 +207,7 @@
 
         return carry
 
-    lax.fori_loop(0, chunks + n - 1, step, 0)
+    lax.fori_loop(0, chunks + SKEW * (n - 1), step, 0)
 
     local = height * parts
     extra = acc1[...] / local
@@ -219,11 +241,11 @@
         g = to
         for hop in range(1, half):
             peer = lax.rem(b + 2 * hop, nb)
-            strip_copy(g, b, w2_send.at[off, hop], w2_recv.at[g, b], {"batch": peer}).wait_send()
+            strip_copy(g, b, w2_send.at[g, hop], w2_recv.at[g, b], {"batch": peer}).wait_send()
         for hop in range(half):
             peer = lax.rem(b + 2 * hop, nb)
             strip_copy(
-                g, peer, w3_send.at[off, hop], w3_recv.at[g, peer], {"batch": partner}
+                g, peer, w3_send.at[g, hop], w3_recv.at[g, peer], {"batch": partner}
             ).wait_send()
 
     def drain(k, carry):
@@ -358,13 +380,6 @@
     lax.fori_loop(0, n * parts, drain, 0)
 
 
-def parts_of(rows):
-    for parts in (7, 4, 2):
-        if rows % (parts * 16) == 0:
-            return parts
-    return 1
-
-
 def body(
     images,
     reduce_weight,
@@ -378,18 +393,16 @@
     expand_bias,
 ):
     imgs, side = (images.shape[0], images.shape[1])
-    rows = imgs * side * side
     n, nb = lax.axis_size("chan"), lax.axis_size("batch")
     mid_local = reduce_weight.shape[1]
     mid = mid_local * n
     depth = images.shape[3]
     out_local = expand_weight.shape[1]
-    parts = parts_of(rows)
-    height = rows // parts
+    parts, height = side, side * imgs
     chunks = n * parts
     dma, f32, bf16 = pltpu.SemaphoreType.DMA, jnp.float32, jnp.bfloat16
     vmem = pl.BlockSpec(memory_space=pltpu.VMEM)
-    flat = images.reshape(parts, height, depth)
+    flat = images.transpose(1, 2, 0, 3).reshape(parts, height, depth)
     act_one = pl.pallas_call(
         functools.partial(first_kernel, n, nb, parts),
         out_shape=jax.ShapeDtypeStruct((parts, height, mid), bf16),
@@ -413,11 +426,11 @@
         name="first",
     )(flat, reduce_weight, jnp.stack([reduce_gain, reduce_bias]))
     second = lax.conv_general_dilated(
-        act_one.reshape(imgs, side, side, mid),
+        act_one.reshape(side, side, imgs, mid),
         spatial_weight,
         (1, 1),
         ((1, 1), (1, 1)),
-        dimension_numbers=("NHWC", "HWIO", "NHWC"),
+        dimension_numbers=("HWNC", "HWIO", "HWNC"),
         preferred_element_type=f32,
     )
     third, norm = pl.pallas_call(
@@ -445,9 +458,9 @@
         expand_weight,
         expand_gain[None, :],
     )
-    normed = (third.reshape(rows, out_local) - norm[0]) * norm[1] + expand_bias
-    summed = normed + images.reshape(rows, out_local).astype(f32)
-    return jnp.maximum(summed, 0.0).astype(bf16).reshape(imgs, side, side, out_local)
+    normed = (third - norm[0]) * norm[1] + expand_bias
+    out = jnp.maximum(normed + flat.astype(f32), 0.0).astype(bf16)
+    return out.reshape(side, side, imgs, out_local).transpose(2, 0, 1, 3)
 
 
 def solution(mesh):

time: 269 us -> 201 us (0.75)
  Pallas kernels: 217 us -> 179 us
  local copies, waits for them, and re-layouts: 27.1 us -> 0.79 us
  other arithmetic: 13.2 us -> 9.46 us
    pallas_call x1, Pallas kernels: 148 us -> 108 us  [body(): pl.pallas_call(functools.partial(first_kernel, n, nb, parts), out_shape=j...]
    reshape x4 -> x0, local copies, waits for them, and re-layouts: 20.3 us -> none  [the longest x1 7.71 us: body(): normed = (third.reshape(rows, out_local) - norm[0]) * norm[1] + expand_bias]
    convert_element_type x1 -> x0, other arithmetic: 10.6 us -> none  [body(): jnp.maximum(summed, 0.0).astype(bf16).reshape(imgs, side, side, out_local)]
    transpose x0 -> x1, other arithmetic: none -> 6.9 us  [body(): return out.reshape(side, side, imgs, out_local).transpose(2, 0, 1, 3)]
    unnamed x5 -> x2, local copies, waits for them, and re-layouts: 5.49 us -> 0.01 us
where the time goes in v2:
time: 201 us
  Pallas kernels  179 us (89%)
  matrix products  11.2 us (6%)
  other arithmetic  9.46 us (5%)
    pallas_call x1, Pallas kernels, body(): pl.pallas_call(functools.partial(first_kernel, n, nb, parts), out_shape=j...  108 us
    pallas_call x1, Pallas kernels, body(): pl.pallas_call(functools.partial(third_kernel, n, nb), out_shape=(jax.Sha...  70.7 us
    conv_general_dilated x1, matrix products, body(): lax.conv_general_dilated(act_one.reshape(side, side, imgs, mid), spatial_...  11.2 us
    transpose x1, other arithmetic, body(): return out.reshape(side, side, imgs, out_local).transpose(2, 0, 1, 3)  6.9 us

profile of v2, /device:TPU:0, one launch (start us, length us, event | category | flops | bytes accessed | tf_op | source)
XLA Modules:
  0.0 200.6 jit_solution(212840683955637611)
XLA Ops:
  0.0 1.3 pad_maximum_fusion.gb_ref
  1.3 1.3 pad_maximum_fusion.1.gb_ref
  2.6 108.3 %first.1 = bf16[14,112,1024]{2,1,0:T(8,128)(2,1)} custom-call(bf16[14,112,1024]{2,1,0:T(8,128)(2,1)} %bitcast.23, bf16[4096,256]{1,0:T(8,128)(2,1)} %w_ref.2, f32[2,256]{1,0:T(2,128)} %pad_maximum_fusion.gb_ref), custom_call_target="tpu_custom_call" | custom-call | tf_op jit(solution)/shard_map/first/pallas_call | solution.py:406
  110.9 0.0 copy-start
  110.9 11.2 %fusion.3.sec_ref = f32[14,112,256]{2,1,0:T(8,128)} fusion(bf16[3,3,1024,256]{3,2,1,0:T(8,128)(2,1)} %param.14, bf16[14,112,1024]{2,1,0:T(8,128)(2,1)} %first.1), kind=kOutput, calls=%fused_computation.4 | convolution fusion | flops 6710886400 | bytes 9535488 | tf_op jit(solution)/shard_map/conv_general_dilated | solution.py:428
  122.2 70.7 %third.1 = (f32[14,112,1024]{2,1,0:T(8,128)}, f32[2,1024]{1,0:T(2,128)}) custom-call(f32[14,112,256]{2,1,0:T(8,128)} %fusion.3.sec_ref, f32[2,256]{1,0:T(2,128)} %pad_maximum_fusion.1.gb_ref, bf16[1024,1024]{1,0:T(8,128)(2,1)} %w_ref.3, f32[1,1024]{1,0:T(1,128)} %bitcast.26), custom_call_target="tpu_custom_call" | custom-call | tf_op jit(solution)/shard_map/third/pallas_call | solution.py:436
  192.9 0.8 fusion.6
  193.7 0.0 copy-done
  193.7 6.9 %fusion = bf16[8,14,14,1024]{3,0,2,1:T(8,128)(2,1)} fusion(f32[14,112,1024]{2,1,0:T(8,128)} %get-tuple-element.7, f32[1024]{0:T(1024)S(1)} %copy-done, f32[1024]{0:T(1024)S(1)} %bitcast.25, f32[1024]{0:T(1024)S(1)} %bitcast.24, bf16[8,14,14,1024]{3,0,2,1:T(8,128)(2,1)} %param.10), kind=kLoop, calls=%fused_computation.1 | loop fusion | flops 11239424 | bytes 12857344 | tf_op jit(solution)/shard_map/transpose | solution.py:463
Async XLA Ops:
  110.9 82.7 %copy-start = (f32[1024]{0:T(1024)S(1)}, f32[1024]{0:T(1024)}, u32[]{:S(2)}) copy-start(f32[1024]{0:T(1024)} %param.19) | copy-start | bytes 12292

commit v3 on v2

--- a/solution.py
+++ b/solution.py
@@ -263,23 +263,31 @@
 
 
 def third_kernel(
-    n, nb, sec_ref, gb_ref, w_ref, gain_ref, out_ref, norm_ref,
-    act, stat2, stat3,
-    right_send, left_send, recv, s2_send, s2_recv, s3_send, s3_recv,
+    n, nb, imgs, one_ref, sw_ref, gb_ref, w_ref, gain_ref, out_ref, norm_ref,
+    pad, act, shift, acc1, acc2, stat2, affine, stat3,
+    right_send, left_send, recv, s2_send, s2_recv, af_send, af_recv, s3_send, s3_recv,
 ):
     z, b = lax.axis_index("chan"), lax.axis_index("batch")
-    parts, height, width = sec_ref.shape
-    local = parts * height
+    side, height, mid = one_ref.shape
+    parts, tall, width = act.shape[1:]
+    join = side // parts
+    local = parts * tall
+    pad[:, 0] = jnp.zeros_like(pad[:, 0])
+    pad[:, side + 1] = jnp.zeros_like(pad[:, 0])
+
+    def spread(r, carry):
+        row = one_ref[r]
+        wide = row.astype(jnp.float32)
+        edge = jnp.zeros((imgs, mid), jnp.float32)
+        pad[1, r + 1] = row
+        pad[0, r + 1] = jnp.concatenate([edge, wide[:-imgs]], axis=0).astype(jnp.bfloat16)
+        pad[2, r + 1] = jnp.concatenate([wide[imgs:], edge], axis=0).astype(jnp.bfloat16)
+        return carry
+
+    lax.fori_loop(0, side, spread, 0)
+    acc1[...] = jnp.zeros_like(acc1)
+    acc2[...] = jnp.zeros_like(acc2)
     greet(n, nb, z, b)
-    values = sec_ref[...]
-    own = jnp.sum(jnp.sum(values, axis=0), axis=0, keepdims=True) / local
-    away = values - own[None]
-    stat2[b, 0:1, :] = own
-    stat2[b, 1:2, :] = jnp.sum(jnp.sum(away * away, axis=0), axis=0, keepdims=True)
-    share_stats(nb, b, stat2, s2_send, s2_recv)
-    mean, var = combine(stat2[...], local)
-    scale = gb_ref[0:1, :] / jnp.sqrt(var + eps)
-    bias = gb_ref[1:2, :]
 
     def right_copy(g, r):
         ref = act.at[g, r]
@@ -296,9 +304,23 @@
     def rows_of(g):
         return pl.ds(pl.multiple_of(g * width, 128), width)
 
-    def begin(r, carry):
-        value = (sec_ref[r] - mean) * scale + bias
-        act[z, r] = jnp.maximum(value, 0.0).astype(jnp.bfloat16)
+    def convolve(r, carry):
+        total = jnp.zeros((tall, width), jnp.float32)
+        for row_tap in range(3):
+            for col_tap in range(3):
+                window = pad[col_tap, pl.ds(r * join + row_tap, join)].reshape(tall, mid)
+                total = total + jnp.dot(
+                    window, sw_ref[row_tap, col_tap], preferred_element_type=jnp.float32
+                )
+
+        @pl.when(r == 0)
+        def _():
+            shift[...] = jnp.sum(total, axis=0, keepdims=True) / tall
+
+        moved = total - shift[...]
+        acc1[...] += jnp.sum(moved, axis=0, keepdims=True)
+        acc2[...] += jnp.sum(moved * moved, axis=0, keepdims=True)
+        act[z, r] = moved.astype(jnp.bfloat16)
 
         @pl.when(z < n - 1)
         def _():
@@ -308,14 +330,40 @@
         def _():
             left_copy(z, r).start()
 
-        out_ref[r] = jnp.dot(act[z, r], w_ref[rows_of(z), :], preferred_element_type=jnp.float32)
-        return carry
-
-    lax.fori_loop(0, parts, begin, 0)
+        return carry
+
+    lax.fori_loop(0, parts, convolve, 0)
+    extra = acc1[...] / local
+    stat2[b, 0:1, :] = shift[...] + extra
+    stat2[b, 1:2, :] = acc2[...] - acc1[...] * extra
+    share_stats(nb, b, stat2, s2_send, s2_recv)
+    mean, var = combine(stat2[...], local)
+    scale = gb_ref[0:1, :] / jnp.sqrt(var + eps)
+    affine[z, 0:1, :] = scale
+    affine[z, 1:2, :] = (shift[...] - mean) * scale + gb_ref[1:2, :]
+
+    def affine_copy(off, slot):
+        to = lax.rem(z + off, n)
+        return remote(
+            affine.at[z], affine.at[slot], af_send.at[off], af_recv.at[slot], {"chan": to}
+        )
+
+    for off in range(1, n):
+        affine_copy(off, z).start()
+    for off in range(1, n):
+        affine_copy(off, lax.rem(z + off, n)).wait()
+
+    def product(g, r):
+        value = act[g, r].astype(jnp.float32) * affine[g, 0:1, :] + affine[g, 1:2, :]
+        return jnp.dot(
+            jnp.maximum(value, 0.0).astype(jnp.bfloat16),
+            w_ref[rows_of(g), :],
+            preferred_element_type=jnp.float32,
+        )
 
     def relay(s, carry):
         d, r = lax.div(s, parts) + 1, lax.rem(s, parts)
-        g = z - d
+        g, h = z - d, z + d
 
         @pl.when(g >= 0)
         def _():
@@ -325,12 +373,6 @@
             def _():
                 right_copy(g, r).start()
 
-            out_ref[r] += jnp.dot(
-                act[g, r], w_ref[rows_of(g), :], preferred_element_type=jnp.float32
-            )
-
-        h = z + d
-
         @pl.when(h < n)
         def _():
             left_copy(h, r).wait_recv()
@@ -339,26 +381,36 @@
             def _():
                 left_copy(h, r).start()
 
-            out_ref[r] += jnp.dot(
-                act[h, r], w_ref[rows_of(h), :], preferred_element_type=jnp.float32
-            )
+        @pl.when(d == 1)
+        def _():
+            out_ref[r] = product(z, r)
+
+        @pl.when(g >= 0)
+        def _():
+            out_ref[r] += product(g, r)
+
+        @pl.when(h < n)
+        def _():
+            out_ref[r] += product(h, r)
 
         return carry
 
     lax.fori_loop(0, parts * (n - 1), relay, 0)
 
+    base = jnp.sum(out_ref[0], axis=0, keepdims=True) / tall
+
     def add(r, carry):
-        return carry + jnp.sum(out_ref[r], axis=0, keepdims=True)
+        moved = out_ref[r] - base
+        return (
+            carry[0] + jnp.sum(moved, axis=0, keepdims=True),
+            carry[1] + jnp.sum(moved * moved, axis=0, keepdims=True),
+        )
 
     zero = jnp.zeros((1, out_ref.shape[2]), jnp.float32)
-    own3 = lax.fori_loop(0, parts, add, zero) / local
-
-    def add_square(r, carry):
-        away = out_ref[r] - own3
-        return carry + jnp.sum(away * away, axis=0, keepdims=True)
-
-    stat3[b, 0:1, :] = own3
-    stat3[b, 1:2, :] = lax.fori_loop(0, parts, add_square, zero)
+    one3, two3 = lax.fori_loop(0, parts, add, (zero, zero))
+    extra3 = one3 / local
+    stat3[b, 0:1, :] = base + extra3
+    stat3[b, 1:2, :] = two3 - one3 * extra3
     share_stats(nb, b, stat3, s3_send, s3_recv)
     mean3, var3 = combine(stat3[...], local)
     norm_ref[0:1, :] = mean3
@@ -425,39 +477,42 @@
         ),
         name="first",
     )(flat, reduce_weight, jnp.stack([reduce_gain, reduce_bias]))
-    second = lax.conv_general_dilated(
-        act_one.reshape(side, side, imgs, mid),
-        spatial_weight,
-        (1, 1),
-        ((1, 1), (1, 1)),
-        dimension_numbers=("HWNC", "HWIO", "HWNC"),
-        preferred_element_type=f32,
-    )
+    join = 2 if side % 2 == 0 else 1
+    pieces, tall = side // join, height * join
     third, norm = pl.pallas_call(
-        functools.partial(third_kernel, n, nb),
+        functools.partial(third_kernel, n, nb, imgs),
         out_shape=(
-            jax.ShapeDtypeStruct((parts, height, out_local), f32),
+            jax.ShapeDtypeStruct((pieces, tall, out_local), f32),
             jax.ShapeDtypeStruct((2, out_local), f32),
         ),
-        in_specs=[vmem] * 4,
+        in_specs=[vmem] * 5,
         out_specs=(vmem, vmem),
         scratch_shapes=[
-            pltpu.VMEM((n, parts, height, mid_local), bf16),
+            pltpu.VMEM((3, side + 2, height, mid), bf16),
+            pltpu.VMEM((n, pieces, tall, mid_local), bf16),
+        ]
+        + [pltpu.VMEM((1, mid_local), f32)] * 3
+        + [
             pltpu.VMEM((nb, 2, mid_local), f32),
+            pltpu.VMEM((n, 2, mid_local), f32),
             pltpu.VMEM((nb, 2, out_local), f32),
         ]
-        + [dma((n, parts))] * 3
-        + [dma((nb,))] * 4,
+        + [dma((n, pieces))] * 3
+        + [dma((nb,))] * 2
+        + [dma((n,))] * 2
+        + [dma((nb,))] * 2,
         compiler_params=pltpu.CompilerParams(
             collective_id=1, has_side_effects=True, vmem_limit_bytes=LIMIT
         ),
         name="third",
     )(
-        second.reshape(parts, height, mid_local),
+        act_one,
+        spatial_weight,
         jnp.stack([spatial_gain, spatial_bias]),
         expand_weight,
         expand_gain[None, :],
     )
+    third = third.reshape(side, height, out_local)
     normed = (third - norm[0]) * norm[1] + expand_bias
     out = jnp.maximum(normed + flat.astype(f32), 0.0).astype(bf16)
     return out.reshape(side, side, imgs, out_local).transpose(2, 0, 1, 3)

time: 201 us -> 191 us (0.950)
  matrix products: 11.2 us -> 0 us
    conv_general_dilated x1 -> x0, matrix products: 11.2 us -> none  [body(): lax.conv_general_dilated(act_one.reshape(side, side, imgs, mid), spatial_...]
where the time goes in v3:
time: 191 us
  Pallas kernels  181 us (95%)
  other arithmetic  9.47 us (5%)
    pallas_call x1, Pallas kernels, body(): pl.pallas_call(functools.partial(first_kernel, n, nb, parts), out_shape=j...  108 us
    pallas_call x1, Pallas kernels, body(): pl.pallas_call(functools.partial(third_kernel, n, nb, imgs), out_shape=(j...  72.1 us
    transpose x1, other arithmetic, body(): return out.reshape(side, side, imgs, out_local).transpose(2, 0, 1, 3)  6.9 us

profile of v3, /device:TPU:0, one launch (start us, length us, event | category | flops | bytes accessed | tf_op | source)
XLA Modules:
  0.0 190.8 jit_solution(9060375606132721641)
XLA Ops:
  0.0 1.3 pad_maximum_fusion.gb_ref
  1.3 1.3 pad_maximum_fusion.1.gb_ref
  2.6 108.4 %first.1.one_ref = bf16[14,112,1024]{2,1,0:T(8,128)(2,1)} custom-call(bf16[14,112,1024]{2,1,0:T(8,128)(2,1)} %bitcast.14, bf16[4096,256]{1,0:T(8,128)(2,1)} %w_ref.2, f32[2,256]{1,0:T(2,128)} %pad_maximum_fusion.gb_ref), custom_call_target="tpu_custom_call" | custom-call | tf_op jit(solution)/shard_map/first/pallas_call | solution.py:458
  111.0 0.0 copy-start
  111.0 72.1 %third.1 = (f32[7,224,1024]{2,1,0:T(8,128)}, f32[2,1024]{1,0:T(2,128)}) custom-call(bf16[14,112,1024]{2,1,0:T(8,128)(2,1)} %first.1.one_ref, bf16[3,3,1024,256]{3,2,1,0:T(8,128)(2,1)} %sw_ref.1, f32[2,256]{1,0:T(2,128)} %pad_maximum_fusion.1.gb_ref, bf16[1024,1024]{1,0:T(8,128)(2,1)} %w_ref.3, f32[1,1024]{1,0:T(1,128)} %bitcast.18), custom_call_target="tpu_custom_call" | custom-call | tf_op jit(solution)/shard_map/third/pallas_call | solution.py:482
  183.1 0.8 fusion.1
  183.9 0.0 copy-done
  183.9 6.9 %fusion = bf16[8,14,14,1024]{3,0,2,1:T(8,128)(2,1)} fusion(f32[14,14,8,1024]{3,2,1,0:T(8,128)} %bitcast.15, bf16[8,14,14,1024]{3,0,2,1:T(8,128)(2,1)} %param.10, f32[1024]{0:T(1024)S(1)} %copy-done, f32[1024]{0:T(1024)S(1)} %bitcast.17, f32[1024]{0:T(1024)S(1)} %bitcast.16), kind=kLoop, calls=%fused_computation.1 | loop fusion | flops 11239424 | bytes 12857344 | tf_op jit(solution)/shard_map/transpose | solution.py:518
Async XLA Ops:
  111.0 72.9 %copy-start = (f32[1024]{0:T(1024)S(1)}, f32[1024]{0:T(1024)}, u32[]{:S(2)}) copy-start(f32[1024]{0:T(1024)} %param.19) | copy-start | bytes 12292

commit v4 on v3

--- a/solution.py
+++ b/solution.py
@@ -56,8 +56,8 @@
 
 
 def first_kernel(
-    n, nb, parts, img_ref, w_ref, gb_ref, out_ref,
-    wown, part, pre_in, suf_in, pre_out, suf_out, gb_in, shift, acc1, acc2, stat_in,
+    n, nb, parts, img_hbm, w_ref, gain_ref, bias_ref, out_ref,
+    img_ref, img_sem, wown, part, pre_in, suf_in, pre_out, suf_out, gb_in, shift, acc1, acc2, stat_in,
     w1_send, w1_recv, w2_send, w2_recv, w3_send, w3_recv, gb_send, gb_recv,
     pre_send, pre_recv, suf_send, suf_recv, st_send, st_recv,
 ):
@@ -69,6 +69,10 @@
     chunks = n * parts
     partner = b + 1 - 2 * lax.rem(b, 2)
     parity = lax.rem(b, 2)
+    img_load = pltpu.make_async_copy(img_hbm, img_ref, img_sem)
+    img_load.start()
+    gb_in[z, 0:1, :] = gain_ref[...]
+    gb_in[z, 1:2, :] = bias_ref[...]
     greet(n, nb, z, b)
 
     def rows_of(who):
@@ -80,10 +84,9 @@
         remote(
             src, wown.at[z, rows_of(b), :], w1_send.at[off], w1_recv.at[z], {"chan": to}
         ).start()
-    gb_in[z] = gb_ref[...]
     for off in range(1, n):
         to = lax.rem(z + off, n)
-        remote(gb_ref, gb_in.at[z], gb_send.at[off], gb_recv.at[z], {"chan": to}).start()
+        remote(gb_in.at[z], gb_in.at[z], gb_send.at[off], gb_recv.at[z], {"chan": to}).start()
 
     wown[z] = w_ref[pl.ds(pl.multiple_of(z * depth, 16), depth), :]
 
@@ -131,6 +134,7 @@
                 ).wait_recv()
 
     forward(0)
+    img_load.wait()
 
     def right_copy(k):
         return remote(
@@ -216,7 +220,7 @@
     share_stats(nb, b, stat_in, st_send, st_recv)
     for off in range(1, n):
         g = lax.rem(z + off, n)
-        remote(gb_ref, gb_in.at[g], gb_send.at[off], gb_recv.at[g], {"chan": g}).wait()
+        remote(gb_in.at[z], gb_in.at[g], gb_send.at[off], gb_recv.at[g], {"chan": g}).wait()
     mean, var = combine(stat_in[...], local)
     scale = gb_in[:, 0:1, :] / jnp.sqrt(var + eps)
     bias = gb_in[:, 1:2, :]
@@ -263,8 +267,8 @@
 
 
 def third_kernel(
-    n, nb, imgs, one_ref, sw_ref, gb_ref, w_ref, gain_ref, out_ref, norm_ref,
-    pad, act, shift, acc1, acc2, stat2, affine, stat3,
+    n, nb, imgs, one_ref, sw_hbm, mid_gain, mid_bias, w_hbm, gain_ref, out_ref, mean_ref, scale_ref,
+    sw_ref, w_ref, sw_sem, w_sem, pad, act, shift, acc1, acc2, stat2, affine, stat3,
     right_send, left_send, recv, s2_send, s2_recv, af_send, af_recv, s3_send, s3_recv,
 ):
     z, b = lax.axis_index("chan"), lax.axis_index("batch")
@@ -272,6 +276,10 @@
     parts, tall, width = act.shape[1:]
     join = side // parts
     local = parts * tall
+    sw_load = pltpu.make_async_copy(sw_hbm, sw_ref, sw_sem)
+    sw_load.start()
+    w_load = pltpu.make_async_copy(w_hbm, w_ref, w_sem)
+    w_load.start()
     pad[:, 0] = jnp.zeros_like(pad[:, 0])
     pad[:, side + 1] = jnp.zeros_like(pad[:, 0])
 
@@ -288,6 +296,8 @@
     acc1[...] = jnp.zeros_like(acc1)
     acc2[...] = jnp.zeros_like(acc2)
     greet(n, nb, z, b)
+    sw_load.wait()
+    w_load.wait()
 
     def right_copy(g, r):
         ref = act.at[g, r]
@@ -338,9 +348,9 @@
     stat2[b, 1:2, :] = acc2[...] - acc1[...] * extra
     share_stats(nb, b, stat2, s2_send, s2_recv)
     mean, var = combine(stat2[...], local)
-    scale = gb_ref[0:1, :] / jnp.sqrt(var + eps)
+    scale = mid_gain[...] / jnp.sqrt(var + eps)
     affine[z, 0:1, :] = scale
-    affine[z, 1:2, :] = (shift[...] - mean) * scale + gb_ref[1:2, :]
+    affine[z, 1:2, :] = (shift[...] - mean) * scale + mid_bias[...]
 
     def affine_copy(off, slot):
         to = lax.rem(z + off, n)
@@ -413,8 +423,8 @@
     stat3[b, 1:2, :] = two3 - one3 * extra3
     share_stats(nb, b, stat3, s3_send, s3_recv)
     mean3, var3 = combine(stat3[...], local)
-    norm_ref[0:1, :] = mean3
-    norm_ref[1:2, :] = gain_ref[...] / jnp.sqrt(var3 + eps)
+    mean_ref[...] = mean3
+    scale_ref[...] = gain_ref[...] / jnp.sqrt(var3 + eps)
 
     def drain(s, carry):
         g, r = lax.div(s, parts), lax.rem(s, parts)
@@ -458,9 +468,11 @@
     act_one = pl.pallas_call(
         functools.partial(first_kernel, n, nb, parts),
         out_shape=jax.ShapeDtypeStruct((parts, height, mid), bf16),
-        in_specs=[vmem] * 3,
+        in_specs=[pl.BlockSpec(memory_space=pl.ANY)] + [vmem] * 3,
         out_specs=vmem,
         scratch_shapes=[
+            pltpu.VMEM((parts, height, depth), bf16),
+            dma,
             pltpu.VMEM((n, depth, mid_local), bf16),
             pltpu.VMEM((chunks, height, mid_local), f32),
         ]
@@ -476,18 +488,24 @@
             collective_id=0, has_side_effects=True, vmem_limit_bytes=LIMIT
         ),
         name="first",
-    )(flat, reduce_weight, jnp.stack([reduce_gain, reduce_bias]))
+    )(flat, reduce_weight, reduce_gain[None, :], reduce_bias[None, :])
+    anywhere = pl.BlockSpec(memory_space=pl.ANY)
     join = 2 if side % 2 == 0 else 1
     pieces, tall = side // join, height * join
-    third, norm = pl.pallas_call(
+    third, mean, scale = pl.pallas_call(
         functools.partial(third_kernel, n, nb, imgs),
         out_shape=(
             jax.ShapeDtypeStruct((pieces, tall, out_local), f32),
-            jax.ShapeDtypeStruct((2, out_local), f32),
+            jax.ShapeDtypeStruct((1, out_local), f32),
+            jax.ShapeDtypeStruct((1, out_local), f32),
         ),
-        in_specs=[vmem] * 5,
-        out_specs=(vmem, vmem),
+        in_specs=[vmem, anywhere, vmem, vmem, anywhere, vmem],
+        out_specs=(vmem, vmem, vmem),
         scratch_shapes=[
+            pltpu.VMEM(spatial_weight.shape, bf16),
+            pltpu.VMEM(expand_weight.shape, bf16),
+            dma,
+            dma,
             pltpu.VMEM((3, side + 2, height, mid), bf16),
             pltpu.VMEM((n, pieces, tall, mid_local), bf16),
         ]
@@ -508,12 +526,13 @@
     )(
         act_one,
         spatial_weight,
-        jnp.stack([spatial_gain, spatial_bias]),
+        spatial_gain[None, :],
+        spatial_bias[None, :],
         expand_weight,
         expand_gain[None, :],
     )
     third = third.reshape(side, height, out_local)
-    normed = (third - norm[0]) * norm[1] + expand_bias
+    normed = (third - mean[0]) * scale[0] + expand_bias
     out = jnp.maximum(normed + flat.astype(f32), 0.0).astype(bf16)
     return out.reshape(side, side, imgs, out_local).transpose(2, 0, 1, 3)
 

time: 191 us -> 185 us (0.969)
  Pallas kernels: 181 us -> 178 us
  other arithmetic: 9.47 us -> 6.94 us
    another operation x2 -> x0, other arithmetic: 2.57 us -> none  [the longest x1 1.29 us: body(): jnp.stack([spatial_gain, spatial_bias])]
where the time goes in v4:
time: 185 us
  Pallas kernels  178 us (96%)
  other arithmetic  6.94 us (4%)
    pallas_call x1, Pallas kernels, body(): pl.pallas_call(functools.partial(first_kernel, n, nb, parts), out_shape=j...  107 us
    pallas_call x1, Pallas kernels, body(): pl.pallas_call(functools.partial(third_kernel, n, nb, imgs), out_shape=(j...  70.8 us
    transpose x1, other arithmetic, body(): return out.reshape(side, side, imgs, out_local).transpose(2, 0, 1, 3)  6.94 us

profile of v4, /device:TPU:0, one launch (start us, length us, event | category | flops | bytes accessed | tf_op | source)
XLA Modules:
  0.0 185.3 jit_solution(16690449491027174778)
XLA Ops:
  0.0 107.5 %first.1.one_ref = bf16[14,112,1024]{2,1,0:T(8,128)(2,1)} custom-call(bf16[14,112,1024]{2,1,0:T(8,128)(2,1)} %bitcast.14, bf16[4096,256]{1,0:T(8,128)(2,1)} %w_ref.1, f32[1,256]{1,0:T(1,128)} %bitcast.19, f32[1,256]{1,0:T(1,128)} %bitcast.20), custom_call_target="tpu_custom_call" | custom-call | tf_op jit(solution)/shard_map/first/pallas_call | solution.py:468
  107.5 0.0 copy-start
  107.5 70.8 %third.1 = (f32[7,224,1024]{2,1,0:T(8,128)}, f32[1,1024]{1,0:T(1,128)}, f32[1,1024]{1,0:T(1,128)}) custom-call(bf16[14,112,1024]{2,1,0:T(8,128)(2,1)} %first.1.one_ref, bf16[3,3,1024,256]{3,2,1,0:T(8,128)(2,1)} %sw_hbm.1, f32[1,256]{1,0:T(1,128)} %bitcast.21, f32[1,256]{1,0:T(1,128)} %bitcast.22, bf16[1024,1024]{1,0:T(8,128)(2,1)} %w_hbm.1, f32[1,1024]{1,0:T(1,128)} %bitcast.16), custom_call_target="tpu_custom_call" | custom-call | tf_op jit(solution)/shard_map/third/pallas_call | solution.py:495
  178.3 0.0 copy-done
  178.4 6.9 %fusion = bf16[8,14,14,1024]{3,0,2,1:T(8,128)(2,1)} fusion(f32[14,14,8,1024]{3,2,1,0:T(8,128)} %bitcast.15, bf16[8,14,14,1024]{3,0,2,1:T(8,128)(2,1)} %param.10, f32[1024]{0:T(1024)S(1)} %copy-done, f32[1024]{0:T(1024)} %bitcast.18, f32[1024]{0:T(1024)} %bitcast.17), kind=kLoop, calls=%fused_computation.1 | loop fusion | flops 11239424 | bytes 12857344 | tf_op jit(solution)/shard_map/transpose | solution.py:537
Async XLA Ops:
  107.5 70.9 %copy-start = (f32[1024]{0:T(1024)S(1)}, f32[1024]{0:T(1024)}, u32[]{:S(2)}) copy-start(f32[1024]{0:T(1024)} %param.19) | copy-start | bytes 12292
